TPU v7x, 32 devices: a whole 2x2x4 slice. The times are simulated.
32 devices in a mesh: slab: 2 (over core), py: 4 (over z), pz: 4 (over y, x).
Axes of the slice: x: 2, y: 2, z: 4, core: 2. Of those that a mesh axis runs over, the one named last changes fastest.
Arguments:
- start_vector: float32 [32, 128, 256], P('pz', 'py', 'slab'), may hold values from -6 to 6
- potential: float32 [32, 128, 256], P('pz', 'py', 'slab'), may hold values from 0.5 to 4
Outputs:
- krylov_basis: float32 [6, 32, 128, 256], P(None, 'pz', 'py', 'slab')
- tridiagonal: float32 [2, 5], replicated
All inputs are finite; a program needn't handle non-finite values.
Results may differ from a plain program's by a relative error of at most 0.00012.
Values sent between devices are 32-bit elements; how exact they have to be, the bound alone decides.
A program may use at most 64 MiB of HBM per device.

v0:
```python
import jax
import jax.numpy as jnp
from jax import lax
from jax.sharding import PartitionSpec as P

ITERS = 5
EPSILON = 1e-06


def with_halo(block, sides, width):
    for axis, dim in sides:
        count = lax.axis_size(axis)
        forward = [(i, i + 1) for i in range(count - 1)]
        backward = [(target, source) for source, target in forward]
        low = lax.ppermute(
            lax.slice_in_dim(block, block.shape[dim] - width, None, axis=dim), axis, forward
        )
        high = lax.ppermute(lax.slice_in_dim(block, 0, width, axis=dim), axis, backward)
        block = jnp.concatenate([low, block, high], axis=dim)
    return block


def apply_hamiltonian(field, potential):
    padded = with_halo(field, (("slab", 2), ("py", 1), ("pz", 0)), 1)
    beside = padded[2:, 1:-1, 1:-1] + padded[:-2, 1:-1, 1:-1]
    beside = beside + padded[1:-1, 2:, 1:-1] + padded[1:-1, :-2, 1:-1]
    beside = beside + padded[1:-1, 1:-1, 2:] + padded[1:-1, 1:-1, :-2]
    return (6.0 + potential) * field - beside


def reduce_all(partials):
    inner = lax.psum(partials, "pz")
    return lax.psum(inner, ("slab", "py"))


def project(active, image):
    return jnp.einsum("kzyx,zyx->k", active, image, precision=lax.Precision.HIGHEST)


def remove(image, coeffs, active):
    return image - jnp.einsum("k,kzyx->zyx", coeffs, active, precision=lax.Precision.HIGHEST)


def shards(start_vector, potential):
    cell_count = (
        start_vector.size * lax.axis_size("slab") * lax.axis_size("py") * lax.axis_size("pz")
    )
    per_cell = jnp.float32(1.0 / cell_count)
    start_norm = reduce_all(jnp.sum(start_vector * start_vector).reshape(1))[0] * per_cell
    vectors = [start_vector / jnp.sqrt(start_norm + EPSILON)]
    alphas = []
    beta_list = []
    for iteration in range(ITERS):
        image = apply_hamiltonian(vectors[-1], potential)
        active = jnp.stack(vectors)
        first_coeff = reduce_all(project(active, image)) * per_cell
        image = remove(image, first_coeff, active)
        local_second = project(active, image)
        summed = (
            reduce_all(jnp.concatenate([local_second, jnp.sum(image * image).reshape(1)]))
            * per_cell
        )
        second_coeff = summed[:-1]
        image = remove(image, second_coeff, active)
        square_mean = summed[-1] - jnp.sum(second_coeff * second_coeff)
        beta_value = jnp.sqrt(square_mean + EPSILON)
        alphas.append(first_coeff[iteration] + second_coeff[iteration])
        beta_list.append(beta_value)
        vectors.append(image / beta_value)
    return (jnp.stack(vectors), jnp.stack([jnp.stack(alphas), jnp.stack(beta_list)]))


def solution(mesh):
    in_specs = (P("pz", "py", "slab"), P("pz", "py", "slab"))
    out_specs = (P(None, "pz", "py", "slab"), P())
    return jax.shard_map(shards, mesh=mesh, in_specs=in_specs, out_specs=out_specs, check_vma=False)
```

profile of v0, /device:TPU:0, one launch (start us, length us, event | category | flops | bytes accessed | tf_op | source)
XLA Modules:
  0.0 438.7 jit_solution(16922644488798986109)
XLA Ops:
  0.6 1.6 multiply_reduce_fusion.7
  2.2 12.0 %psum.154 = f32[1]{0:T(128)} all-reduce(f32[1]{0:T(128)} %bitcast.4), channel_id=1, replica_groups=mesh['slab'=2,'py'=4,'pz'=4] {'pz'}, use_global_device_ids=true, to_apply=%region_1.0 | all-reduce | flops 1 | bytes 8 | tf_op jit(solution)/shard_map/psum | solution.py:32
  14.2 16.0 %psum.155 = f32[1]{0:T(128)} all-reduce(f32[1]{0:T(128)} %psum.154), channel_id=1, replica_groups=mesh['slab'=2,'py'=4,'pz'=4] {'slab','py'}, use_global_device_ids=true, to_apply=%region_2.0 | all-reduce | flops 1 | bytes 8 | tf_op jit(solution)/shard_map/psum | solution.py:33
  31.1 3.9 collective-permute-start
  36.3 1.9 collective-permute-done.1
  39.7 1.4 collective-permute-start.3
  41.1 4.2 collective-permute-done.3
  45.5 1.5 collective-permute-start.5
  48.7 4.6 %collective-permute-done.4 = f32[1,34,130]{2,1,0:T(8,128)S(1)} collective-permute-done((f32[1,34,130]{2,1,0:T(8,128)S(1)}, f32[1,34,130]{2,1,0:T(8,128)S(1)}, u32[]{:S(2)}, u32[]{:S(2)}) %collective-permute-start.4) | collective-permute-done | bytes 17712 | tf_op jit(solution)/shard_map/ppermute | solution.py:18
  54.2 11.0 %psum.156 = f32[1]{0:T(128)} all-reduce(f32[1]{0:T(128)} %bitcast.7), channel_id=1, replica_groups=mesh['slab'=2,'py'=4,'pz'=4] {'pz'}, use_global_device_ids=true, to_apply=%region_3.0 | all-reduce | flops 1 | bytes 8 | tf_op jit(solution)/shard_map/psum | solution.py:32
  65.2 14.7 %psum.157 = f32[1]{0:T(128)} all-reduce(f32[1]{0:T(128)} %psum.156), channel_id=1, replica_groups=mesh['slab'=2,'py'=4,'pz'=4] {'slab','py'}, use_global_device_ids=true, to_apply=%region_4.0 | all-reduce | flops 1 | bytes 8 | tf_op jit(solution)/shard_map/psum | solution.py:33
  81.9 1.4 pad_maximum_fusion.134
  83.3 7.4 %psum.158 = f32[2]{0:T(128)S(1)} all-reduce(f32[2]{0:T(128)S(1)} %pad_maximum_fusion.134), channel_id=1, replica_groups=mesh['slab'=2,'py'=4,'pz'=4] {'pz'}, use_global_device_ids=true, to_apply=%region_6.0 | all-reduce | flops 2 | bytes 16 | tf_op jit(solution)/shard_map/psum | solution.py:32
  90.7 15.6 %psum.159 = f32[2]{0:T(128)S(1)} all-reduce(f32[2]{0:T(128)S(1)} %psum.158), channel_id=1, replica_groups=mesh['slab'=2,'py'=4,'pz'=4] {'slab','py'}, use_global_device_ids=true, to_apply=%region_7.0 | all-reduce | flops 2 | bytes 16 | tf_op jit(solution)/shard_map/psum | solution.py:33
  109.8 2.0 collective-permute-start.6
  113.1 1.9 collective-permute-done.7
  115.2 1.5 collective-permute-start.8
  118.1 4.2 collective-permute-done.9
  122.4 3.9 collective-permute-start.11
  128.0 4.2 collective-permute-done.10
  132.5 2.4 convolution_bitcast_fusion.5
  135.0 9.3 %psum.160 = f32[2]{0:T(128)S(1)} all-reduce(f32[2]{0:T(128)S(1)} %convolution_bitcast_fusion.5), channel_id=1, replica_groups=mesh['slab'=2,'py'=4,'pz'=4] {'pz'}, use_global_device_ids=true, to_apply=%region_8.0 | all-reduce | flops 2 | bytes 16 | tf_op jit(solution)/shard_map/psum | solution.py:32
  144.2 14.4 %psum.161 = f32[2]{0:T(128)S(1)} all-reduce(f32[2]{0:T(128)S(1)} %psum.160), channel_id=1, replica_groups=mesh['slab'=2,'py'=4,'pz'=4] {'slab','py'}, use_global_device_ids=true, to_apply=%region_9.0 | all-reduce | flops 2 | bytes 16 | tf_op jit(solution)/shard_map/psum | solution.py:33
  160.3 2.4 convolution_bitcast_fusion.4
  163.3 8.5 %psum.162 = f32[3]{0:T(128)S(1)} all-reduce(f32[3]{0:T(128)S(1)} %pad_maximum_fusion.135), channel_id=1, replica_groups=mesh['slab'=2,'py'=4,'pz'=4] {'pz'}, use_global_device_ids=true, to_apply=%region_11.0 | all-reduce | flops 3 | bytes 24 | tf_op jit(solution)/shard_map/psum | solution.py:32
  171.8 15.2 %psum.163 = f32[3]{0:T(128)S(1)} all-reduce(f32[3]{0:T(128)S(1)} %psum.162), channel_id=1, replica_groups=mesh['slab'=2,'py'=4,'pz'=4] {'slab','py'}, use_global_device_ids=true, to_apply=%region_12.0 | all-reduce | flops 3 | bytes 24 | tf_op jit(solution)/shard_map/psum | solution.py:33
  190.7 2.0 collective-permute-start.12
  194.1 1.9 collective-permute-done.13
  196.1 1.9 collective-permute-start.14
  199.4 4.2 collective-permute-done.15
  203.7 2.9 collective-permute-start.17
  208.2 4.2 collective-permute-done.16
  212.8 2.4 convolution_bitcast_fusion.3
  215.2 9.4 %psum.164 = f32[3]{0:T(128)S(1)} all-reduce(f32[3]{0:T(128)S(1)} %convolution_bitcast_fusion.3), channel_id=1, replica_groups=mesh['slab'=2,'py'=4,'pz'=4] {'pz'}, use_global_device_ids=true, to_apply=%region_14.0 | all-reduce | flops 3 | bytes 24 | tf_op jit(solution)/shard_map/psum | solution.py:32
  224.6 14.2 %psum.165 = f32[3]{0:T(128)S(1)} all-reduce(f32[3]{0:T(128)S(1)} %psum.164), channel_id=1, replica_groups=mesh['slab'=2,'py'=4,'pz'=4] {'slab','py'}, use_global_device_ids=true, to_apply=%region_15.0 | all-reduce | flops 3 | bytes 24 | tf_op jit(solution)/shard_map/psum | solution.py:33
  240.7 2.4 convolution_bitcast_fusion.2
  243.8 8.3 %psum.166 = f32[4]{0:T(128)S(1)} all-reduce(f32[4]{0:T(128)S(1)} %pad_maximum_fusion.136), channel_id=1, replica_groups=mesh['slab'=2,'py'=4,'pz'=4] {'pz'}, use_global_device_ids=true, to_apply=%region_17.0 | all-reduce | flops 4 | bytes 32 | tf_op jit(solution)/shard_map/psum | solution.py:32
  252.1 15.6 %psum.167 = f32[4]{0:T(128)S(1)} all-reduce(f32[4]{0:T(128)S(1)} %psum.166), channel_id=1, replica_groups=mesh['slab'=2,'py'=4,'pz'=4] {'slab','py'}, use_global_device_ids=true, to_apply=%region_18.0 | all-reduce | flops 4 | bytes 32 | tf_op jit(solution)/shard_map/psum | solution.py:33
  271.5 2.0 collective-permute-start.18
  274.8 1.9 collective-permute-done.19
  276.9 1.5 collective-permute-start.20
  279.8 4.2 collective-permute-done.21
  284.1 3.1 collective-permute-start.23
  288.8 4.2 collective-permute-done.22
  293.4 2.6 convolution_bitcast_fusion.1
  295.9 9.3 %psum.168 = f32[4]{0:T(128)S(1)} all-reduce(f32[4]{0:T(128)S(1)} %convolution_bitcast_fusion.1), channel_id=1, replica_groups=mesh['slab'=2,'py'=4,'pz'=4] {'pz'}, use_global_device_ids=true, to_apply=%region_20.0 | all-reduce | flops 4 | bytes 32 | tf_op jit(solution)/shard_map/psum | solution.py:32
  305.2 14.4 %psum.169 = f32[4]{0:T(128)S(1)} all-reduce(f32[4]{0:T(128)S(1)} %psum.168), channel_id=1, replica_groups=mesh['slab'=2,'py'=4,'pz'=4] {'slab','py'}, use_global_device_ids=true, to_apply=%region_21.0 | all-reduce | flops 4 | bytes 32 | tf_op jit(solution)/shard_map/psum | solution.py:33
  321.5 2.6 convolution_bitcast_fusion
  325.4 8.5 %psum.170 = f32[5]{0:T(128)S(1)} all-reduce(f32[5]{0:T(128)S(1)} %pad_maximum_fusion.137), channel_id=1, replica_groups=mesh['slab'=2,'py'=4,'pz'=4] {'pz'}, use_global_device_ids=true, to_apply=%region_23.0 | all-reduce | flops 5 | bytes 40 | tf_op jit(solution)/shard_map/psum | solution.py:32
  333.9 15.2 %psum.171 = f32[5]{0:T(128)S(1)} all-reduce(f32[5]{0:T(128)S(1)} %psum.170), channel_id=1, replica_groups=mesh['slab'=2,'py'=4,'pz'=4] {'slab','py'}, use_global_device_ids=true, to_apply=%region_24.0 | all-reduce | flops 5 | bytes 40 | tf_op jit(solution)/shard_map/psum | solution.py:33
  353.0 2.0 collective-permute-start.24
  358.4 1.9 collective-permute-start.26
  360.3 1.5 collective-permute-start.27
  361.8 4.0 collective-permute-done.27
  365.9 2.9 collective-permute-start.29
  372.0 2.7 collective-permute-done.28
  375.1 2.5 fusion.8
  377.6 9.4 %psum.172 = f32[5]{0:T(128)S(1)} all-reduce(f32[5]{0:T(128)S(1)} %fusion.8), channel_id=1, replica_groups=mesh['slab'=2,'py'=4,'pz'=4] {'pz'}, use_global_device_ids=true, to_apply=%region_26.0 | all-reduce | flops 5 | bytes 40 | tf_op jit(solution)/shard_map/psum | solution.py:32
  387.0 14.0 %psum.173 = f32[5]{0:T(128)S(1)} all-reduce(f32[5]{0:T(128)S(1)} %psum.172), channel_id=1, replica_groups=mesh['slab'=2,'py'=4,'pz'=4] {'slab','py'}, use_global_device_ids=true, to_apply=%region_27.0 | all-reduce | flops 5 | bytes 40 | tf_op jit(solution)/shard_map/psum | solution.py:33
  401.0 1.3 fusion.2
  403.0 2.5 fusion.11
  406.8 8.3 %psum.174 = f32[6]{0:T(128)S(1)} all-reduce(f32[6]{0:T(128)S(1)} %pad_maximum_fusion.138), channel_id=1, replica_groups=mesh['slab'=2,'py'=4,'pz'=4] {'pz'}, use_global_device_ids=true, to_apply=%region_29.0 | all-reduce | flops 6 | bytes 48 | tf_op jit(solution)/shard_map/psum | solution.py:32
  416.4 15.6 %psum.175 = f32[6]{0:T(128)S(1)} all-reduce(f32[6]{0:T(128)S(1)} %psum.174), channel_id=1, replica_groups=mesh['slab'=2,'py'=4,'pz'=4] {'slab','py'}, use_global_device_ids=true, to_apply=%region_30.0 | all-reduce | flops 6 | bytes 48 | tf_op jit(solution)/shard_map/psum | solution.py:33
  432.0 1.3 fusion
  (110 shorter events, 46.9 us)
Async XLA Ops:
  0.6 30.3 %copy-start.1 = (f32[8,32,128]{2,1,0:T(8,128)S(1)}, f32[8,32,128]{2,1,0:T(8,128)}, u32[]{:S(2)}) copy-start(f32[8,32,128]{2,1,0:T(8,128)} %param.2) | copy-start | bytes 393220
  31.1 5.2 %collective-permute-start = (f32[8,32,1]{2,1,0:T(8,128)S(1)}, f32[8,32,1]{2,1,0:T(8,128)S(1)}, u32[]{:S(2)}, u32[]{:S(2)}) collective-permute-start(f32[8,32,1]{2,1,0:T(8,128)S(1)} %get-tuple-element.52), channel_id=1, source_target_pairs={{0,16},{1,17},{2,18},{3,19},{4,20},{5,21},{6,22},{7,23},{8,24},{9,... | collective-permute-start | bytes 3080 | tf_op jit(solution)/shard_map/ppermute | solution.py:15
  35.0 3.2 collective-permute-start.1
  38.4 2.7 collective-permute-start.2
  39.7 13.6 %copy-start = (f32[8,32,128]{2,1,0:T(8,128)S(1)}, f32[8,32,128]{2,1,0:T(8,128)}, u32[]{:S(2)}) copy-start(f32[8,32,128]{2,1,0:T(8,128)} %param.3) | copy-start | bytes 393220
  39.7 5.7 %collective-permute-start.3 = (f32[8,1,130]{2,1,0:T(1,128)S(1)}, f32[8,1,130]{2,1,0:T(1,128)S(1)}, u32[]{:S(2)}, u32[]{:S(2)}) collective-permute-start(f32[8,1,130]{2,1,0:T(1,128)S(1)} %get-tuple-element.40), channel_id=1, source_target_pairs={{4,0},{8,4},{12,8},{5,1},{9,5},{13,9},{6,2},{10,6},{14,10},{7,3},{... | collective-permute-start | bytes 12488 | tf_op jit(solution)/shard_map/ppermute | solution.py:18
  45.5 3.2 collective-permute-start.5
  47.0 6.3 %collective-permute-start.4 = (f32[1,34,130]{2,1,0:T(8,128)S(1)}, f32[1,34,130]{2,1,0:T(8,128)S(1)}, u32[]{:S(2)}, u32[]{:S(2)}) collective-permute-start(f32[1,34,130]{2,1,0:T(8,128)S(1)} %get-tuple-element.30), channel_id=1, source_target_pairs={{1,0},{2,1},{3,2},{5,4},{6,5},{7,6},{9,8},{10,9},{11,10},{13,12},{... | collective-permute-start | bytes 53048 | tf_op jit(solution)/shard_map/ppermute | solution.py:18
  109.8 3.3 collective-permute-start.6
  111.8 3.2 collective-permute-start.7
  115.2 2.9 collective-permute-start.8
  116.7 5.5 %collective-permute-start.9 = (f32[8,1,130]{2,1,0:T(1,128)S(1)}, f32[8,1,130]{2,1,0:T(1,128)S(1)}, u32[]{:S(2)}, u32[]{:S(2)}) collective-permute-start(f32[8,1,130]{2,1,0:T(1,128)S(1)} %get-tuple-element.38), channel_id=1, source_target_pairs={{4,0},{8,4},{12,8},{5,1},{9,5},{13,9},{6,2},{10,6},{14,10},{7,3},{... | collective-permute-start | bytes 12488 | tf_op jit(solution)/shard_map/ppermute | solution.py:18
  122.4 5.6 %collective-permute-start.11 = (f32[1,34,130]{2,1,0:T(8,128)S(1)}, f32[1,34,130]{2,1,0:T(8,128)S(1)}, u32[]{:S(2)}, u32[]{:S(2)}) collective-permute-start(f32[1,34,130]{2,1,0:T(8,128)S(1)} %get-tuple-element.29), channel_id=1, source_target_pairs={{0,1},{1,2},{2,3},{4,5},{5,6},{6,7},{8,9},{9,10},{10,11},{12,13},{... | collective-permute-start | bytes 53048 | tf_op jit(solution)/shard_map/ppermute | solution.py:15
  126.3 5.9 %collective-permute-start.10 = (f32[1,34,130]{2,1,0:T(8,128)S(1)}, f32[1,34,130]{2,1,0:T(8,128)S(1)}, u32[]{:S(2)}, u32[]{:S(2)}) collective-permute-start(f32[1,34,130]{2,1,0:T(8,128)S(1)} %get-tuple-element.28), channel_id=1, source_target_pairs={{1,0},{2,1},{3,2},{5,4},{6,5},{7,6},{9,8},{10,9},{11,10},{13,12},{... | collective-permute-start | bytes 53048 | tf_op jit(solution)/shard_map/ppermute | solution.py:18
  190.7 3.3 collective-permute-start.12
  192.8 3.2 collective-permute-start.13
  196.1 3.2 collective-permute-start.14
  198.0 5.5 %collective-permute-start.15 = (f32[8,1,130]{2,1,0:T(1,128)S(1)}, f32[8,1,130]{2,1,0:T(1,128)S(1)}, u32[]{:S(2)}, u32[]{:S(2)}) collective-permute-start(f32[8,1,130]{2,1,0:T(1,128)S(1)} %get-tuple-element.36), channel_id=1, source_target_pairs={{4,0},{8,4},{12,8},{5,1},{9,5},{13,9},{6,2},{10,6},{14,10},{7,3},{... | collective-permute-start | bytes 12488 | tf_op jit(solution)/shard_map/ppermute | solution.py:18
  203.7 4.6 %collective-permute-start.17 = (f32[1,34,130]{2,1,0:T(8,128)S(1)}, f32[1,34,130]{2,1,0:T(8,128)S(1)}, u32[]{:S(2)}, u32[]{:S(2)}) collective-permute-start(f32[1,34,130]{2,1,0:T(8,128)S(1)} %get-tuple-element.27), channel_id=1, source_target_pairs={{0,1},{1,2},{2,3},{4,5},{5,6},{6,7},{8,9},{9,10},{10,11},{12,13},{... | collective-permute-start | bytes 53048 | tf_op jit(solution)/shard_map/ppermute | solution.py:15
  206.6 5.9 %collective-permute-start.16 = (f32[1,34,130]{2,1,0:T(8,128)S(1)}, f32[1,34,130]{2,1,0:T(8,128)S(1)}, u32[]{:S(2)}, u32[]{:S(2)}) collective-permute-start(f32[1,34,130]{2,1,0:T(8,128)S(1)} %get-tuple-element.26), channel_id=1, source_target_pairs={{1,0},{2,1},{3,2},{5,4},{6,5},{7,6},{9,8},{10,9},{11,10},{13,12},{... | collective-permute-start | bytes 53048 | tf_op jit(solution)/shard_map/ppermute | solution.py:18
  271.5 3.3 collective-permute-start.18
  273.5 3.2 collective-permute-start.19
  276.9 2.9 collective-permute-start.20
  278.4 5.5 %collective-permute-start.21 = (f32[8,1,130]{2,1,0:T(1,128)S(1)}, f32[8,1,130]{2,1,0:T(1,128)S(1)}, u32[]{:S(2)}, u32[]{:S(2)}) collective-permute-start(f32[8,1,130]{2,1,0:T(1,128)S(1)} %get-tuple-element.34), channel_id=1, source_target_pairs={{4,0},{8,4},{12,8},{5,1},{9,5},{13,9},{6,2},{10,6},{14,10},{7,3},{... | collective-permute-start | bytes 12488 | tf_op jit(solution)/shard_map/ppermute | solution.py:18
  284.1 4.7 %collective-permute-start.23 = (f32[1,34,130]{2,1,0:T(8,128)S(1)}, f32[1,34,130]{2,1,0:T(8,128)S(1)}, u32[]{:S(2)}, u32[]{:S(2)}) collective-permute-start(f32[1,34,130]{2,1,0:T(8,128)S(1)} %get-tuple-element.25), channel_id=1, source_target_pairs={{0,1},{1,2},{2,3},{4,5},{5,6},{6,7},{8,9},{9,10},{10,11},{12,13},{... | collective-permute-start | bytes 53048 | tf_op jit(solution)/shard_map/ppermute | solution.py:15
  287.1 5.9 %collective-permute-start.22 = (f32[1,34,130]{2,1,0:T(8,128)S(1)}, f32[1,34,130]{2,1,0:T(8,128)S(1)}, u32[]{:S(2)}, u32[]{:S(2)}) collective-permute-start(f32[1,34,130]{2,1,0:T(8,128)S(1)} %get-tuple-element.24), channel_id=1, source_target_pairs={{1,0},{2,1},{3,2},{5,4},{6,5},{7,6},{9,8},{10,9},{11,10},{13,12},{... | collective-permute-start | bytes 53048 | tf_op jit(solution)/shard_map/ppermute | solution.py:18
  353.0 5.2 %collective-permute-start.24 = (f32[8,32,1]{2,1,0:T(8,128)S(1)}, f32[8,32,1]{2,1,0:T(8,128)S(1)}, u32[]{:S(2)}, u32[]{:S(2)}) collective-permute-start(f32[8,32,1]{2,1,0:T(8,128)S(1)} %get-tuple-element.43), channel_id=1, source_target_pairs={{0,16},{1,17},{2,18},{3,19},{4,20},{5,21},{6,22},{7,23},{8,24},{9,... | collective-permute-start | bytes 3080 | tf_op jit(solution)/shard_map/ppermute | solution.py:15
  355.0 3.2 collective-permute-start.25
  358.4 3.4 collective-permute-start.26
  360.3 5.5 %collective-permute-start.27 = (f32[8,1,130]{2,1,0:T(1,128)S(1)}, f32[8,1,130]{2,1,0:T(1,128)S(1)}, u32[]{:S(2)}, u32[]{:S(2)}) collective-permute-start(f32[8,1,130]{2,1,0:T(1,128)S(1)} %get-tuple-element.32), channel_id=1, source_target_pairs={{4,0},{8,4},{12,8},{5,1},{9,5},{13,9},{6,2},{10,6},{14,10},{7,3},{... | collective-permute-start | bytes 12488 | tf_op jit(solution)/shard_map/ppermute | solution.py:18
  365.9 6.1 %collective-permute-start.29 = (f32[1,34,130]{2,1,0:T(8,128)S(1)}, f32[1,34,130]{2,1,0:T(8,128)S(1)}, u32[]{:S(2)}, u32[]{:S(2)}) collective-permute-start(f32[1,34,130]{2,1,0:T(8,128)S(1)} %get-tuple-element.23), channel_id=1, source_target_pairs={{0,1},{1,2},{2,3},{4,5},{5,6},{6,7},{8,9},{9,10},{10,11},{12,13},{... | collective-permute-start | bytes 53048 | tf_op jit(solution)/shard_map/ppermute | solution.py:15
  368.8 5.9 %collective-permute-start.28 = (f32[1,34,130]{2,1,0:T(8,128)S(1)}, f32[1,34,130]{2,1,0:T(8,128)S(1)}, u32[]{:S(2)}, u32[]{:S(2)}) collective-permute-start(f32[1,34,130]{2,1,0:T(8,128)S(1)} %get-tuple-element.22), channel_id=1, source_target_pairs={{1,0},{2,1},{3,2},{5,4},{6,5},{7,6},{9,8},{10,9},{11,10},{13,12},{... | collective-permute-start | bytes 53048 | tf_op jit(solution)/shard_map/ppermute | solution.py:18
  437.8 0.9 copy-start.2
where the time goes:
time: 440 us; the launch traced here: 439 us
  blocking collectives  266 us (60%)
  starting transfers between devices  54.2 us (12%)
  waiting for transfers between devices  50.1 us (11%)
  matrix products  29.2 us (7%)
  other arithmetic  17.2 us (4%)
  between operations  15.6 us (4%)
  local copies, waits for them, and re-layouts  6.18 us (1%)
    psum x11, blocking collectives, reduce_all(): return lax.psum(inner, ('slab', 'py'))  165 us
    psum x11, blocking collectives, reduce_all(): inner = lax.psum(partials, 'pz')  101 us
    ppermute x15, waiting for transfers between devices, with_halo(): lax.ppermute(lax.slice_in_dim(block, 0, width, axis=dim), axis, backward)  48.7 us
    ppermute x15, starting transfers between devices, with_halo(): lax.ppermute(lax.slice_in_dim(block, block.shape[dim] - width, None, axis...  34.5 us
    ppermute x15, starting transfers between devices, with_halo(): lax.ppermute(lax.slice_in_dim(block, 0, width, axis=dim), axis, backward)  19.7 us
    dot_general x8, matrix products, project(): jnp.einsum('kzyx,zyx->k', active, image, precision=lax.Precision.HIGHEST)  19.6 us
    dot_general x8, matrix products, remove(): jnp.einsum('k,kzyx->zyx', coeffs, active, precision=lax.Precision.HIGHEST)  9.56 us
  transfers between devices with their start and end apart: 30, of which 19 were waited for; matrix products, arithmetic and copies ran while one was open for 0% of the time, Pallas kernels for 0%

commit v1 on v0

--- a/solution.py
+++ b/solution.py
@@ -30,7 +30,7 @@
 
 def reduce_all(partials):
     inner = lax.psum(partials, "pz")
-    return lax.psum(inner, ("slab", "py"))
+    return jax.lax.psum(jax.lax.psum(inner, "py"), "slab")
 
 
 def project(active, image):

time: 440 us -> 413 us (0.939)
  blocking collectives: 266 us -> 237 us
    psum x11 -> x22, blocking collectives: 165 us -> 135 us  [reduce_all(): return jax.lax.psum(jax.lax.psum(inner, 'py'), 'slab')]
  transfers between devices with their start and end apart: 30 -> 30, of which waited for: 19 -> 20; matrix products, arithmetic and copies ran while one was open for 0% -> 0% of each run, Pallas kernels for 0% -> 0%
where the time goes in v1:
time: 413 us; the launch traced here: 411 us
  blocking collectives  237 us (57%)
  starting transfers between devices  54 us (13%)
  waiting for transfers between devices  52.2 us (13%)
  matrix products  29.2 us (7%)
  other arithmetic  17.2 us (4%)
  between operations  15.6 us (4%)
  local copies, waits for them, and re-layouts  6.18 us (1%)
    psum x22, blocking collectives, reduce_all(): return jax.lax.psum(jax.lax.psum(inner, 'py'), 'slab')  135 us
    psum x11, blocking collectives, reduce_all(): inner = lax.psum(partials, 'pz')  101 us
    ppermute x15, waiting for transfers between devices, with_halo(): lax.ppermute(lax.slice_in_dim(block, 0, width, axis=dim), axis, backward)  50.4 us
    ppermute x15, starting transfers between devices, with_halo(): lax.ppermute(lax.slice_in_dim(block, block.shape[dim] - width, None, axis...  34.5 us
    dot_general x8, matrix products, project(): jnp.einsum('kzyx,zyx->k', active, image, precision=lax.Precision.HIGHEST)  19.6 us
    ppermute x15, starting transfers between devices, with_halo(): lax.ppermute(lax.slice_in_dim(block, 0, width, axis=dim), axis, backward)  19.5 us
    dot_general x8, matrix products, remove(): jnp.einsum('k,kzyx->zyx', coeffs, active, precision=lax.Precision.HIGHEST)  9.57 us
  transfers between devices with their start and end apart: 30, of which 20 were waited for; matrix products, arithmetic and copies ran while one was open for 0% of the time, Pallas kernels for 0%

profile of v1, /device:TPU:0, one launch (start us, length us, event | category | flops | bytes accessed | tf_op | source)
XLA Modules:
  0.0 411.0 jit_solution(12547723713136495679)
XLA Ops:
  2.2 12.0 %psum.231 = f32[1]{0:T(128)} all-reduce(f32[1]{0:T(128)} %bitcast.4), channel_id=1, replica_groups=mesh['slab'=2,'py'=4,'pz'=4] {'pz'}, use_global_device_ids=true, to_apply=%region_1.0 | all-reduce | flops 1 | bytes 8 | tf_op jit(solution)/shard_map/psum | solution.py:32
  14.2 12.6 %psum.232 = f32[1]{0:T(128)} all-reduce(f32[1]{0:T(128)} %psum.231), channel_id=1, replica_groups=mesh['slab'=2,'py'=4,'pz'=4] {'py'}, use_global_device_ids=true, to_apply=%region_2.0 | all-reduce | flops 1 | bytes 8 | tf_op jit(solution)/shard_map/psum | solution.py:33
  26.8 3.1 psum.233
  30.7 2.1 collective-permute-start
  34.1 1.9 collective-permute-done.1
  38.9 4.2 %collective-permute-done.3 = f32[8,1,130]{2,1,0:T(1,128)S(1)} collective-permute-done((f32[8,1,130]{2,1,0:T(1,128)S(1)}, f32[8,1,130]{2,1,0:T(1,128)S(1)}, u32[]{:S(2)}, u32[]{:S(2)}) %collective-permute-start.3) | collective-permute-done | bytes 4192 | tf_op jit(solution)/shard_map/ppermute | solution.py:18
  46.5 4.6 %collective-permute-done.4 = f32[1,34,130]{2,1,0:T(8,128)S(1)} collective-permute-done((f32[1,34,130]{2,1,0:T(8,128)S(1)}, f32[1,34,130]{2,1,0:T(8,128)S(1)}, u32[]{:S(2)}, u32[]{:S(2)}) %collective-permute-start.4) | collective-permute-done | bytes 17712 | tf_op jit(solution)/shard_map/ppermute | solution.py:18
  52.0 11.0 %psum.234 = f32[1]{0:T(128)} all-reduce(f32[1]{0:T(128)} %bitcast.7), channel_id=1, replica_groups=mesh['slab'=2,'py'=4,'pz'=4] {'pz'}, use_global_device_ids=true, to_apply=%region_4.0 | all-reduce | flops 1 | bytes 8 | tf_op jit(solution)/shard_map/psum | solution.py:32
  63.0 9.8 %psum.235 = f32[1]{0:T(128)} all-reduce(f32[1]{0:T(128)} %psum.234), channel_id=1, replica_groups=mesh['slab'=2,'py'=4,'pz'=4] {'py'}, use_global_device_ids=true, to_apply=%region_5.0 | all-reduce | flops 1 | bytes 8 | tf_op jit(solution)/shard_map/psum | solution.py:33
  72.8 3.1 psum.236
  79.3 7.4 %psum.237 = f32[2]{0:T(128)S(1)} all-reduce(f32[2]{0:T(128)S(1)} %pad_maximum_fusion.134), channel_id=1, replica_groups=mesh['slab'=2,'py'=4,'pz'=4] {'pz'}, use_global_device_ids=true, to_apply=%region_8.0 | all-reduce | flops 2 | bytes 16 | tf_op jit(solution)/shard_map/psum | solution.py:32
  86.7 9.6 %psum.238 = f32[2]{0:T(128)S(1)} all-reduce(f32[2]{0:T(128)S(1)} %psum.237), channel_id=1, replica_groups=mesh['slab'=2,'py'=4,'pz'=4] {'py'}, use_global_device_ids=true, to_apply=%region_9.0 | all-reduce | flops 2 | bytes 16 | tf_op jit(solution)/shard_map/psum | solution.py:33
  96.3 2.5 psum.239
  102.2 2.1 collective-permute-start.6
  105.6 1.9 collective-permute-done.7
  107.7 2.7 collective-permute-start.8
  111.7 4.2 %collective-permute-done.9 = f32[8,1,130]{2,1,0:T(1,128)S(1)} collective-permute-done((f32[8,1,130]{2,1,0:T(1,128)S(1)}, f32[8,1,130]{2,1,0:T(1,128)S(1)}, u32[]{:S(2)}, u32[]{:S(2)}) %collective-permute-start.9) | collective-permute-done | bytes 4192 | tf_op jit(solution)/shard_map/ppermute | solution.py:18
  116.0 3.9 collective-permute-start.11
  121.6 4.2 %collective-permute-done.10 = f32[1,34,130]{2,1,0:T(8,128)S(1)} collective-permute-done((f32[1,34,130]{2,1,0:T(8,128)S(1)}, f32[1,34,130]{2,1,0:T(8,128)S(1)}, u32[]{:S(2)}, u32[]{:S(2)}) %collective-permute-start.10) | collective-permute-done | bytes 17712 | tf_op jit(solution)/shard_map/ppermute | solution.py:18
  126.2 2.4 convolution_bitcast_fusion.5
  128.6 9.3 %psum.240 = f32[2]{0:T(128)S(1)} all-reduce(f32[2]{0:T(128)S(1)} %convolution_bitcast_fusion.5), channel_id=1, replica_groups=mesh['slab'=2,'py'=4,'pz'=4] {'pz'}, use_global_device_ids=true, to_apply=%region_11.0 | all-reduce | flops 2 | bytes 16 | tf_op jit(solution)/shard_map/psum | solution.py:32
  137.8 8.4 %psum.241 = f32[2]{0:T(128)S(1)} all-reduce(f32[2]{0:T(128)S(1)} %psum.240), channel_id=1, replica_groups=mesh['slab'=2,'py'=4,'pz'=4] {'py'}, use_global_device_ids=true, to_apply=%region_12.0 | all-reduce | flops 2 | bytes 16 | tf_op jit(solution)/shard_map/psum | solution.py:33
  146.2 2.5 psum.242
  150.3 2.4 convolution_bitcast_fusion.4
  153.4 8.5 %psum.243 = f32[3]{0:T(128)S(1)} all-reduce(f32[3]{0:T(128)S(1)} %pad_maximum_fusion.135), channel_id=1, replica_groups=mesh['slab'=2,'py'=4,'pz'=4] {'pz'}, use_global_device_ids=true, to_apply=%region_15.0 | all-reduce | flops 3 | bytes 24 | tf_op jit(solution)/shard_map/psum | solution.py:32
  161.9 10.3 %psum.244 = f32[3]{0:T(128)S(1)} all-reduce(f32[3]{0:T(128)S(1)} %psum.243), channel_id=1, replica_groups=mesh['slab'=2,'py'=4,'pz'=4] {'py'}, use_global_device_ids=true, to_apply=%region_16.0 | all-reduce | flops 3 | bytes 24 | tf_op jit(solution)/shard_map/psum | solution.py:33
  172.2 2.5 psum.245
  178.4 2.1 collective-permute-start.12
  187.1 4.2 %collective-permute-done.15 = f32[8,1,130]{2,1,0:T(1,128)S(1)} collective-permute-done((f32[8,1,130]{2,1,0:T(1,128)S(1)}, f32[8,1,130]{2,1,0:T(1,128)S(1)}, u32[]{:S(2)}, u32[]{:S(2)}) %collective-permute-start.15) | collective-permute-done | bytes 4192 | tf_op jit(solution)/shard_map/ppermute | solution.py:18
  191.4 2.9 collective-permute-start.17
  195.9 4.2 %collective-permute-done.16 = f32[1,34,130]{2,1,0:T(8,128)S(1)} collective-permute-done((f32[1,34,130]{2,1,0:T(8,128)S(1)}, f32[1,34,130]{2,1,0:T(8,128)S(1)}, u32[]{:S(2)}, u32[]{:S(2)}) %collective-permute-start.16) | collective-permute-done | bytes 17712 | tf_op jit(solution)/shard_map/ppermute | solution.py:18
  200.5 2.4 convolution_bitcast_fusion.3
  202.9 9.4 %psum.246 = f32[3]{0:T(128)S(1)} all-reduce(f32[3]{0:T(128)S(1)} %convolution_bitcast_fusion.3), channel_id=1, replica_groups=mesh['slab'=2,'py'=4,'pz'=4] {'pz'}, use_global_device_ids=true, to_apply=%region_19.0 | all-reduce | flops 3 | bytes 24 | tf_op jit(solution)/shard_map/psum | solution.py:32
  212.3 8.7 %psum.247 = f32[3]{0:T(128)S(1)} all-reduce(f32[3]{0:T(128)S(1)} %psum.246), channel_id=1, replica_groups=mesh['slab'=2,'py'=4,'pz'=4] {'py'}, use_global_device_ids=true, to_apply=%region_20.0 | all-reduce | flops 3 | bytes 24 | tf_op jit(solution)/shard_map/psum | solution.py:33
  221.1 2.5 psum.248
  225.4 2.4 convolution_bitcast_fusion.2
  228.4 8.3 %psum.249 = f32[4]{0:T(128)S(1)} all-reduce(f32[4]{0:T(128)S(1)} %pad_maximum_fusion.136), channel_id=1, replica_groups=mesh['slab'=2,'py'=4,'pz'=4] {'pz'}, use_global_device_ids=true, to_apply=%region_23.0 | all-reduce | flops 4 | bytes 32 | tf_op jit(solution)/shard_map/psum | solution.py:32
  236.7 10.2 %psum.250 = f32[4]{0:T(128)S(1)} all-reduce(f32[4]{0:T(128)S(1)} %psum.249), channel_id=1, replica_groups=mesh['slab'=2,'py'=4,'pz'=4] {'py'}, use_global_device_ids=true, to_apply=%region_24.0 | all-reduce | flops 4 | bytes 32 | tf_op jit(solution)/shard_map/psum | solution.py:33
  246.9 2.5 psum.251
  253.2 2.1 collective-permute-start.18
  258.6 2.1 collective-permute-start.20
  262.1 4.2 %collective-permute-done.21 = f32[8,1,130]{2,1,0:T(1,128)S(1)} collective-permute-done((f32[8,1,130]{2,1,0:T(1,128)S(1)}, f32[8,1,130]{2,1,0:T(1,128)S(1)}, u32[]{:S(2)}, u32[]{:S(2)}) %collective-permute-start.21) | collective-permute-done | bytes 4192 | tf_op jit(solution)/shard_map/ppermute | solution.py:18
  266.4 3.1 collective-permute-start.23
  271.1 4.2 %collective-permute-done.22 = f32[1,34,130]{2,1,0:T(8,128)S(1)} collective-permute-done((f32[1,34,130]{2,1,0:T(8,128)S(1)}, f32[1,34,130]{2,1,0:T(8,128)S(1)}, u32[]{:S(2)}, u32[]{:S(2)}) %collective-permute-start.22) | collective-permute-done | bytes 17712 | tf_op jit(solution)/shard_map/ppermute | solution.py:18
  275.7 2.6 convolution_bitcast_fusion.1
  278.3 9.3 %psum.252 = f32[4]{0:T(128)S(1)} all-reduce(f32[4]{0:T(128)S(1)} %convolution_bitcast_fusion.1), channel_id=1, replica_groups=mesh['slab'=2,'py'=4,'pz'=4] {'pz'}, use_global_device_ids=true, to_apply=%region_27.0 | all-reduce | flops 4 | bytes 32 | tf_op jit(solution)/shard_map/psum | solution.py:32
  287.5 8.4 %psum.253 = f32[4]{0:T(128)S(1)} all-reduce(f32[4]{0:T(128)S(1)} %psum.252), channel_id=1, replica_groups=mesh['slab'=2,'py'=4,'pz'=4] {'py'}, use_global_device_ids=true, to_apply=%region_28.0 | all-reduce | flops 4 | bytes 32 | tf_op jit(solution)/shard_map/psum | solution.py:33
  295.9 2.5 psum.254
  300.3 2.6 convolution_bitcast_fusion
  303.5 8.5 %psum.255 = f32[5]{0:T(128)S(1)} all-reduce(f32[5]{0:T(128)S(1)} %pad_maximum_fusion.137), channel_id=1, replica_groups=mesh['slab'=2,'py'=4,'pz'=4] {'pz'}, use_global_device_ids=true, to_apply=%region_31.0 | all-reduce | flops 5 | bytes 40 | tf_op jit(solution)/shard_map/psum | solution.py:32
  312.7 10.4 %psum.256 = f32[5]{0:T(128)S(1)} all-reduce(f32[5]{0:T(128)S(1)} %psum.255), channel_id=1, replica_groups=mesh['slab'=2,'py'=4,'pz'=4] {'py'}, use_global_device_ids=true, to_apply=%region_32.0 | all-reduce | flops 5 | bytes 40 | tf_op jit(solution)/shard_map/psum | solution.py:33
  323.1 2.5 psum.257
  329.3 2.1 collective-permute-start.24
  338.0 4.2 %collective-permute-done.27 = f32[8,1,130]{2,1,0:T(1,128)S(1)} collective-permute-done((f32[8,1,130]{2,1,0:T(1,128)S(1)}, f32[8,1,130]{2,1,0:T(1,128)S(1)}, u32[]{:S(2)}, u32[]{:S(2)}) %collective-permute-start.27) | collective-permute-done | bytes 4192 | tf_op jit(solution)/shard_map/ppermute | solution.py:18
  342.3 2.9 collective-permute-start.29
  346.9 4.2 %collective-permute-done.28 = f32[1,34,130]{2,1,0:T(8,128)S(1)} collective-permute-done((f32[1,34,130]{2,1,0:T(8,128)S(1)}, f32[1,34,130]{2,1,0:T(8,128)S(1)}, u32[]{:S(2)}, u32[]{:S(2)}) %collective-permute-start.28) | collective-permute-done | bytes 17712 | tf_op jit(solution)/shard_map/ppermute | solution.py:18
  351.5 2.5 fusion.8
  354.6 9.4 %psum.258 = f32[5]{0:T(128)S(1)} all-reduce(f32[5]{0:T(128)S(1)} %fusion.8), channel_id=1, replica_groups=mesh['slab'=2,'py'=4,'pz'=4] {'pz'}, use_global_device_ids=true, to_apply=%region_35.0 | all-reduce | flops 5 | bytes 40 | tf_op jit(solution)/shard_map/psum | solution.py:32
  365.2 8.6 %psum.259 = f32[5]{0:T(128)S(1)} all-reduce(f32[5]{0:T(128)S(1)} %psum.258), channel_id=1, replica_groups=mesh['slab'=2,'py'=4,'pz'=4] {'py'}, use_global_device_ids=true, to_apply=%region_36.0 | all-reduce | flops 5 | bytes 40 | tf_op jit(solution)/shard_map/psum | solution.py:33
  373.8 2.5 psum.260
  378.3 2.5 fusion.11
  381.5 8.3 %psum.261 = f32[6]{0:T(128)S(1)} all-reduce(f32[6]{0:T(128)S(1)} %pad_maximum_fusion.138), channel_id=1, replica_groups=mesh['slab'=2,'py'=4,'pz'=4] {'pz'}, use_global_device_ids=true, to_apply=%region_39.0 | all-reduce | flops 6 | bytes 48 | tf_op jit(solution)/shard_map/psum | solution.py:32
  390.4 10.1 %psum.262 = f32[6]{0:T(128)S(1)} all-reduce(f32[6]{0:T(128)S(1)} %psum.261), channel_id=1, replica_groups=mesh['slab'=2,'py'=4,'pz'=4] {'py'}, use_global_device_ids=true, to_apply=%region_40.0 | all-reduce | flops 6 | bytes 48 | tf_op jit(solution)/shard_map/psum | solution.py:33
  401.8 2.5 psum.263
  (121 shorter events, 64.8 us)
Async XLA Ops:
  0.6 29.9 %copy-start.1 = (f32[8,32,128]{2,1,0:T(8,128)S(1)}, f32[8,32,128]{2,1,0:T(8,128)}, u32[]{:S(2)}) copy-start(f32[8,32,128]{2,1,0:T(8,128)} %param.2) | copy-start | bytes 393220
  30.7 3.4 collective-permute-start
  32.8 3.2 collective-permute-start.1
  36.2 2.7 collective-permute-start.2
  37.5 13.6 %copy-start = (f32[8,32,128]{2,1,0:T(8,128)S(1)}, f32[8,32,128]{2,1,0:T(8,128)}, u32[]{:S(2)}) copy-start(f32[8,32,128]{2,1,0:T(8,128)} %param.3) | copy-start | bytes 393220
  37.5 5.7 %collective-permute-start.3 = (f32[8,1,130]{2,1,0:T(1,128)S(1)}, f32[8,1,130]{2,1,0:T(1,128)S(1)}, u32[]{:S(2)}, u32[]{:S(2)}) collective-permute-start(f32[8,1,130]{2,1,0:T(1,128)S(1)} %get-tuple-element.40), channel_id=1, source_target_pairs={{4,0},{8,4},{12,8},{5,1},{9,5},{13,9},{6,2},{10,6},{14,10},{7,3},{... | collective-permute-start | bytes 12488 | tf_op jit(solution)/shard_map/ppermute | solution.py:18
  43.3 3.2 collective-permute-start.5
  44.8 6.3 %collective-permute-start.4 = (f32[1,34,130]{2,1,0:T(8,128)S(1)}, f32[1,34,130]{2,1,0:T(8,128)S(1)}, u32[]{:S(2)}, u32[]{:S(2)}) collective-permute-start(f32[1,34,130]{2,1,0:T(8,128)S(1)} %get-tuple-element.30), channel_id=1, source_target_pairs={{1,0},{2,1},{3,2},{5,4},{6,5},{7,6},{9,8},{10,9},{11,10},{13,12},{... | collective-permute-start | bytes 53048 | tf_op jit(solution)/shard_map/ppermute | solution.py:18
  102.2 3.4 collective-permute-start.6
  104.3 3.2 collective-permute-start.7
  107.7 4.0 collective-permute-start.8
  110.3 5.5 %collective-permute-start.9 = (f32[8,1,130]{2,1,0:T(1,128)S(1)}, f32[8,1,130]{2,1,0:T(1,128)S(1)}, u32[]{:S(2)}, u32[]{:S(2)}) collective-permute-start(f32[8,1,130]{2,1,0:T(1,128)S(1)} %get-tuple-element.38), channel_id=1, source_target_pairs={{4,0},{8,4},{12,8},{5,1},{9,5},{13,9},{6,2},{10,6},{14,10},{7,3},{... | collective-permute-start | bytes 12488 | tf_op jit(solution)/shard_map/ppermute | solution.py:18
  116.0 5.6 %collective-permute-start.11 = (f32[1,34,130]{2,1,0:T(8,128)S(1)}, f32[1,34,130]{2,1,0:T(8,128)S(1)}, u32[]{:S(2)}, u32[]{:S(2)}) collective-permute-start(f32[1,34,130]{2,1,0:T(8,128)S(1)} %get-tuple-element.29), channel_id=1, source_target_pairs={{0,1},{1,2},{2,3},{4,5},{5,6},{6,7},{8,9},{9,10},{10,11},{12,13},{... | collective-permute-start | bytes 53048 | tf_op jit(solution)/shard_map/ppermute | solution.py:15
  119.9 5.9 %collective-permute-start.10 = (f32[1,34,130]{2,1,0:T(8,128)S(1)}, f32[1,34,130]{2,1,0:T(8,128)S(1)}, u32[]{:S(2)}, u32[]{:S(2)}) collective-permute-start(f32[1,34,130]{2,1,0:T(8,128)S(1)} %get-tuple-element.28), channel_id=1, source_target_pairs={{1,0},{2,1},{3,2},{5,4},{6,5},{7,6},{9,8},{10,9},{11,10},{13,12},{... | collective-permute-start | bytes 53048 | tf_op jit(solution)/shard_map/ppermute | solution.py:18
  178.4 3.4 collective-permute-start.12
  180.5 3.2 collective-permute-start.13
  183.8 3.2 collective-permute-start.14
  185.7 5.5 %collective-permute-start.15 = (f32[8,1,130]{2,1,0:T(1,128)S(1)}, f32[8,1,130]{2,1,0:T(1,128)S(1)}, u32[]{:S(2)}, u32[]{:S(2)}) collective-permute-start(f32[8,1,130]{2,1,0:T(1,128)S(1)} %get-tuple-element.36), channel_id=1, source_target_pairs={{4,0},{8,4},{12,8},{5,1},{9,5},{13,9},{6,2},{10,6},{14,10},{7,3},{... | collective-permute-start | bytes 12488 | tf_op jit(solution)/shard_map/ppermute | solution.py:18
  191.4 4.6 %collective-permute-start.17 = (f32[1,34,130]{2,1,0:T(8,128)S(1)}, f32[1,34,130]{2,1,0:T(8,128)S(1)}, u32[]{:S(2)}, u32[]{:S(2)}) collective-permute-start(f32[1,34,130]{2,1,0:T(8,128)S(1)} %get-tuple-element.27), channel_id=1, source_target_pairs={{0,1},{1,2},{2,3},{4,5},{5,6},{6,7},{8,9},{9,10},{10,11},{12,13},{... | collective-permute-start | bytes 53048 | tf_op jit(solution)/shard_map/ppermute | solution.py:15
  194.3 5.9 %collective-permute-start.16 = (f32[1,34,130]{2,1,0:T(8,128)S(1)}, f32[1,34,130]{2,1,0:T(8,128)S(1)}, u32[]{:S(2)}, u32[]{:S(2)}) collective-permute-start(f32[1,34,130]{2,1,0:T(8,128)S(1)} %get-tuple-element.26), channel_id=1, source_target_pairs={{1,0},{2,1},{3,2},{5,4},{6,5},{7,6},{9,8},{10,9},{11,10},{13,12},{... | collective-permute-start | bytes 53048 | tf_op jit(solution)/shard_map/ppermute | solution.py:18
  253.2 3.4 collective-permute-start.18
  255.3 3.2 collective-permute-start.19
  258.6 3.4 collective-permute-start.20
  260.7 5.5 %collective-permute-start.21 = (f32[8,1,130]{2,1,0:T(1,128)S(1)}, f32[8,1,130]{2,1,0:T(1,128)S(1)}, u32[]{:S(2)}, u32[]{:S(2)}) collective-permute-start(f32[8,1,130]{2,1,0:T(1,128)S(1)} %get-tuple-element.34), channel_id=1, source_target_pairs={{4,0},{8,4},{12,8},{5,1},{9,5},{13,9},{6,2},{10,6},{14,10},{7,3},{... | collective-permute-start | bytes 12488 | tf_op jit(solution)/shard_map/ppermute | solution.py:18
  266.4 4.7 %collective-permute-start.23 = (f32[1,34,130]{2,1,0:T(8,128)S(1)}, f32[1,34,130]{2,1,0:T(8,128)S(1)}, u32[]{:S(2)}, u32[]{:S(2)}) collective-permute-start(f32[1,34,130]{2,1,0:T(8,128)S(1)} %get-tuple-element.25), channel_id=1, source_target_pairs={{0,1},{1,2},{2,3},{4,5},{5,6},{6,7},{8,9},{9,10},{10,11},{12,13},{... | collective-permute-start | bytes 53048 | tf_op jit(solution)/shard_map/ppermute | solution.py:15
  269.5 5.9 %collective-permute-start.22 = (f32[1,34,130]{2,1,0:T(8,128)S(1)}, f32[1,34,130]{2,1,0:T(8,128)S(1)}, u32[]{:S(2)}, u32[]{:S(2)}) collective-permute-start(f32[1,34,130]{2,1,0:T(8,128)S(1)} %get-tuple-element.24), channel_id=1, source_target_pairs={{1,0},{2,1},{3,2},{5,4},{6,5},{7,6},{9,8},{10,9},{11,10},{13,12},{... | collective-permute-start | bytes 53048 | tf_op jit(solution)/shard_map/ppermute | solution.py:18
  329.3 5.3 %collective-permute-start.24 = (f32[8,32,1]{2,1,0:T(8,128)S(1)}, f32[8,32,1]{2,1,0:T(8,128)S(1)}, u32[]{:S(2)}, u32[]{:S(2)}) collective-permute-start(f32[8,32,1]{2,1,0:T(8,128)S(1)} %get-tuple-element.43), channel_id=1, source_target_pairs={{0,16},{1,17},{2,18},{3,19},{4,20},{5,21},{6,22},{7,23},{8,24},{9,... | collective-permute-start | bytes 3080 | tf_op jit(solution)/shard_map/ppermute | solution.py:15
  331.4 3.2 collective-permute-start.25
  334.8 3.2 collective-permute-start.26
  336.7 5.5 %collective-permute-start.27 = (f32[8,1,130]{2,1,0:T(1,128)S(1)}, f32[8,1,130]{2,1,0:T(1,128)S(1)}, u32[]{:S(2)}, u32[]{:S(2)}) collective-permute-start(f32[8,1,130]{2,1,0:T(1,128)S(1)} %get-tuple-element.32), channel_id=1, source_target_pairs={{4,0},{8,4},{12,8},{5,1},{9,5},{13,9},{6,2},{10,6},{14,10},{7,3},{... | collective-permute-start | bytes 12488 | tf_op jit(solution)/shard_map/ppermute | solution.py:18
  342.3 4.6 %collective-permute-start.29 = (f32[1,34,130]{2,1,0:T(8,128)S(1)}, f32[1,34,130]{2,1,0:T(8,128)S(1)}, u32[]{:S(2)}, u32[]{:S(2)}) collective-permute-start(f32[1,34,130]{2,1,0:T(8,128)S(1)} %get-tuple-element.23), channel_id=1, source_target_pairs={{0,1},{1,2},{2,3},{4,5},{5,6},{6,7},{8,9},{9,10},{10,11},{12,13},{... | collective-permute-start | bytes 53048 | tf_op jit(solution)/shard_map/ppermute | solution.py:15
  345.2 5.9 %collective-permute-start.28 = (f32[1,34,130]{2,1,0:T(8,128)S(1)}, f32[1,34,130]{2,1,0:T(8,128)S(1)}, u32[]{:S(2)}, u32[]{:S(2)}) collective-permute-start(f32[1,34,130]{2,1,0:T(8,128)S(1)} %get-tuple-element.22), channel_id=1, source_target_pairs={{1,0},{2,1},{3,2},{5,4},{6,5},{7,6},{9,8},{10,9},{11,10},{13,12},{... | collective-permute-start | bytes 53048 | tf_op jit(solution)/shard_map/ppermute | solution.py:18
  410.1 0.9 copy-start.2
